TPU v7x, 512 devices: a whole 4x4x16 slice. The times are simulated.
512 devices in a mesh: frow: 32 (over z_lo, y, core), fcol: 16 (over z_hi, x).
Axes of the slice: x: 4, y: 4, z: 16 (z_hi: 4, z_lo: 4; z = z_hi * 4 + z_lo), core: 2. Of those that a mesh axis runs over, the one named last changes fastest.
Arguments:
- model_image: bfloat16 [16384, 16384], P('frow', 'fcol'), may hold values from -6 to 6
- weight_grids: bfloat16 [8, 256, 256], replicated, may hold values from 0.19921875 to 2
- strip_offsets: int32 [2], replicated, may hold values from 0 to 63
- subgrid_offsets: int32 [2, 32], replicated, may hold values from 0 to 63
- grid_index: int32 [2, 32], replicated, may hold values from 0 to 7
Outputs:
- residual_update: float32 [16384, 16384], P('frow', 'fcol')
Inputs may be any that keep to these rules, and one draw needn't show every extreme that they name: `strip_offsets`: two strips may coincide. `subgrid_offsets`: two subgrids of one strip may coincide.
All inputs are finite; a program needn't handle non-finite values.
Results may differ from a plain program's by a relative error of at most 0.03.
Values may be sent and summed in bfloat16 or wider, within the bound.
No kernel may reach another device: no remote copies, remote signals or barrier semaphores. Data moves between devices by JAX's collectives and lax.ppermute only.
A program may use at most 64 MiB of HBM per device.

v0:
```python
import math
import jax
import jax.numpy as jnp
from jax import lax
from jax.sharding import PartitionSpec as P

STRIP = 256


def split_up(value, dim, length):
    dims = value.shape
    parts = value.reshape(*dims[:dim], length, dims[dim] // length, *dims[dim + 1 :])
    return jnp.moveaxis(parts, dim, 0)


def sent_and_summed(value, axis, dim):
    length = lax.axis_size(axis)
    parts = lax.all_to_all(split_up(value, dim, length), axis, 0, 0, tiled=True)
    return jnp.sum(parts.astype(jnp.float32), axis=0)


def joined_along(parts, dim):
    parts = jnp.moveaxis(parts, 0, dim)
    dims = parts.shape
    return parts.reshape(*dims[:dim], dims[dim] * dims[dim + 1], *dims[dim + 2 :])


def copy_for_each(value, axis):
    copies = jnp.broadcast_to(value, (lax.axis_size(axis), *value.shape))
    return lax.all_to_all(copies, axis, split_axis=0, concat_axis=0, tiled=True)


def gathered_copies(value, axis, dim):
    return joined_along(copy_for_each(value, axis), dim)


def phase_pair(leading, trailing, modulus, factor):
    turns = leading[:, None] * trailing[None, :] % modulus
    angle = turns.astype(jnp.float32) * (2.0 * math.pi / modulus)
    return (jnp.cos(angle) * factor, jnp.sin(angle) * factor)


def modulate(strip_real, strip_imag, cos_shift, sin_shift):
    real_part = strip_real[None] * cos_shift[:, None, :] + strip_imag[None] * sin_shift[:, None, :]
    imag_part = strip_imag[None] * cos_shift[:, None, :] - strip_real[None] * sin_shift[:, None, :]
    return jnp.concatenate([real_part, imag_part], axis=2).astype(jnp.bfloat16)


def demodulate(spectra, cos_shift, sin_shift, width):
    real_in = spectra[:, :, :width]
    imag_in = spectra[:, :, width:]
    real_part = jnp.sum(real_in * cos_shift[:, None, :] - imag_in * sin_shift[:, None, :], axis=0)
    imag_part = jnp.sum(imag_in * cos_shift[:, None, :] + real_in * sin_shift[:, None, :], axis=0)
    return jnp.concatenate([real_part, imag_part], axis=1)


def forward_table(pixels, sub_width, modulus, factor):
    spaced = jnp.arange(sub_width, dtype=jnp.int32) * (modulus // sub_width)
    cosine, sine = phase_pair(pixels, spaced, modulus, factor)
    upper = jnp.concatenate([cosine, -sine], axis=1)
    lower = jnp.concatenate([sine, cosine], axis=1)
    return jnp.concatenate([upper, lower], axis=0).astype(jnp.bfloat16)


def backward_table(pixels, sub_width, modulus, factor):
    spaced = jnp.arange(sub_width, dtype=jnp.int32) * (modulus // sub_width)
    cosine, sine = phase_pair(spaced, pixels, modulus, factor)
    upper = jnp.concatenate([cosine, sine], axis=1)
    lower = jnp.concatenate([-sine, cosine], axis=1)
    return jnp.concatenate([upper, lower], axis=0).astype(jnp.bfloat16)


def body(model_image, weight_grids, strip_offsets, subgrid_offsets, grid_index):
    rows_local, facet_width = model_image.shape
    row_groups = lax.axis_size("frow")
    modulus = facet_width * lax.axis_size("fcol")
    uv_rows = strip_offsets.shape[0] * STRIP
    share_rows = uv_rows // row_groups
    sub_width = weight_grids.shape[2]
    subgrid_count = subgrid_offsets.shape[1]
    forward_scale = 1.0 / math.sqrt(modulus)
    column_scale = 1.0 / math.sqrt(subgrid_count * sub_width)
    row_scale = 1.0 / math.sqrt(uv_rows)
    row_index = lax.axis_index("frow")
    pixel_rows = row_index * rows_local + jnp.arange(rows_local, dtype=jnp.int32)
    pixel_cols = lax.axis_index("fcol") * facet_width + jnp.arange(facet_width, dtype=jnp.int32)
    row_spacing = modulus // STRIP
    frequencies = (
        strip_offsets[:, None] + jnp.arange(STRIP, dtype=jnp.int32)[None, :] * row_spacing
    ).reshape(uv_rows)
    wanted = frequencies
    cosine, sine = phase_pair(wanted, pixel_rows, modulus, forward_scale)
    phases = jnp.concatenate([cosine, sine], axis=0).astype(jnp.bfloat16)
    stacked = jnp.dot(phases, model_image, preferred_element_type=jnp.float32)
    mine = sent_and_summed(
        jnp.concatenate(
            [
                stacked[: share_rows * lax.axis_size("frow")],
                -stacked[share_rows * lax.axis_size("frow") :],
            ],
            axis=1,
        ).astype(jnp.bfloat16),
        "frow",
        0,
    )
    strip = mine.astype(jnp.bfloat16)
    strip_real = strip[:, :facet_width]
    strip_imag = strip[:, facet_width:]
    first_global = row_index * share_rows
    strip_number = first_global // STRIP
    strip_row = first_global % STRIP
    my_shifts = lax.dynamic_index_in_dim(subgrid_offsets, strip_number, 0, keepdims=False)
    my_grids = lax.dynamic_index_in_dim(grid_index, strip_number, 0, keepdims=False)
    my_table = lax.dynamic_slice_in_dim(weight_grids, strip_row, share_rows, 1)
    ahead = forward_table(pixel_cols, sub_width, modulus, forward_scale)
    behind = backward_table(pixel_cols, sub_width, modulus, column_scale)
    local_count = subgrid_count // lax.axis_size("fcol")
    shifts = my_shifts
    cos_shift, sin_shift = phase_pair(shifts, pixel_cols, modulus, 1.0)
    modulated = modulate(strip_real, strip_imag, cos_shift, sin_shift)
    flat = modulated.reshape(local_count * lax.axis_size("fcol") * share_rows, 2 * facet_width)
    spectra = jnp.dot(flat, ahead, preferred_element_type=jnp.float32)
    owned = sent_and_summed(
        spectra.reshape(local_count * lax.axis_size("fcol"), share_rows, 2 * sub_width).astype(
            jnp.bfloat16
        ),
        "fcol",
        0,
    )
    chosen = lax.dynamic_slice_in_dim(
        my_grids, lax.axis_index("fcol") * local_count, owned.shape[0]
    )
    grids = jnp.take(my_table, chosen, axis=0).astype(jnp.float32)
    owned_weighted = (owned * jnp.concatenate([grids, grids], axis=2)).astype(jnp.bfloat16)
    shards = gathered_copies(owned_weighted, "fcol", 0)
    shifts = my_shifts
    cos_shift, sin_shift = phase_pair(shifts, pixel_cols, modulus, 1.0)
    flat = shards.reshape(shards.shape[0] * share_rows, 2 * sub_width)
    spectra = jnp.dot(flat, behind, preferred_element_type=jnp.float32)
    spectra = spectra.reshape(shards.shape[0], share_rows, 2 * facet_width)
    merged = demodulate(spectra, cos_shift, sin_shift, facet_width)
    strip_image = merged.astype(jnp.bfloat16)
    shards = lax.all_gather(strip_image, "frow", axis=0, tiled=True)
    wanted = frequencies
    cosine, sine = phase_pair(pixel_rows, wanted, modulus, row_scale)
    phases = jnp.concatenate([cosine, -sine], axis=1).astype(jnp.bfloat16)
    stacked = jnp.concatenate([shards[:, :facet_width], shards[:, facet_width:]], axis=0)
    return jnp.dot(phases, stacked, preferred_element_type=jnp.float32)


def solution(mesh):
    return jax.shard_map(
        body,
        mesh=mesh,
        in_specs=(P("frow", "fcol"), P(), P(), P(), P()),
        out_specs=P("frow", "fcol"),
        check_vma=False,
    )
```

profile of v0, /device:TPU:1, one launch (start us, length us, event | category | flops | bytes accessed | tf_op | source)
XLA Modules:
  0.0 238.4 jit_solution(12703936831153355637)
XLA Ops:
  6.5 0.0 copy-start
  6.5 0.8 add_bitcast_fusion
  7.4 9.9 %multiply_convert_fusion.4 = (bf16[512,512]{1,0:T(8,128)(2,1)}, bf16[512,512]{1,0:T(8,128)(2,1)}, bf16[512,512]{1,0:T(8,128)(2,1)S(1)}, bf16[512,512]{1,0:T(8,128)(2,1)S(1)}) fusion(s32[512]{0:T(512)S(1)} %bitcast.28, s32[512]{0:T(512)S(1)} %iota_add_fusion.1), kind=kLoop, calls=%fused_computation.82 | loop fusion | flops 9699328 | bytes 2101248 | tf_op jit(solution)/shard_map/convert.25
  17.2 0.0 copy-done
  17.2 1.3 fusion.40
  18.5 0.2 slice.53
  18.7 0.3 fusion
  18.9 1.5 pad_maximum_fusion
  20.4 0.0 copy-start.7
  20.4 10.6 %all-to-all-start = ((bf16[32,16,2048]{2,1,0:T(8,128)(2,1)}), bf16[32,16,2048]{2,1,0:T(8,128)(2,1)S(1)}, u32[]{:S(2)}, u32[]{:S(2)}) async-start(bf16[32,16,2048]{2,1,0:T(8,128)(2,1)} %pad_maximum_fusion), calls=%async_computation | async-start | bytes 4194304 | tf_op jit(solution)/shard_map/all_to_all | solution.py:18
  31.1 0.0 copy-done.7
  31.1 0.6 fusion.50
  31.7 5.8 %negate_convert_fusion.1 = (bf16[1024,256]{1,0:T(8,128)(2,1)}, bf16[1024,256]{1,0:T(8,128)(2,1)}, bf16[1024,256]{1,0:T(8,128)(2,1)}) fusion(s32[256]{0:T(256)S(1)} %iota_multiply_fusion, s32[1024]{0:T(1024)S(1)} %iota_add_fusion), kind=kLoop, calls=%fused_computation.76 | loop fusion | flops 5242880 | bytes 1577984 | tf_op jit(solution)/shard_map/convert.15
  37.6 41.6 %all-to-all-done = bf16[32,16,2048]{2,1,0:T(8,128)(2,1)S(1)} async-done(((bf16[32,16,2048]{2,1,0:T(8,128)(2,1)}), bf16[32,16,2048]{2,1,0:T(8,128)(2,1)S(1)}, u32[]{:S(2)}, u32[]{:S(2)}) %all-to-all-start) | async-done | bytes 2097184 | tf_op jit(solution)/shard_map/all_to_all | solution.py:18
  79.2 0.3 reduce_sum.39
  79.5 0.0 copy-start.3
  79.5 0.0 copy-start.4
  79.5 0.0 copy-start.5
  79.5 0.7 add_convert_fusion
  80.3 0.3 copy-done.3
  80.5 0.2 copy-done.4
  80.7 0.2 copy-done.5
  80.8 0.0 copy-start.6
  80.9 2.0 fusion.22
  82.9 14.2 %all-to-all-start.1 = ((bf16[16,2,16,512]{3,2,1,0:T(8,128)(2,1)}), bf16[16,2,16,512]{3,2,1,0:T(8,128)(2,1)S(1)}, u32[]{:S(2)}, u32[]{:S(2)}) async-start(bf16[16,2,16,512]{3,2,1,0:T(8,128)(2,1)} %bitcast.4), calls=%async_computation.1 | async-start | bytes 1048576 | tf_op jit(solution)/shard_map/all_to_all | solution.py:18
  97.2 0.0 copy-done.6
  97.2 0.1 fusion.51
  97.3 0.8 constant_dynamic-slice_fusion
  98.1 0.5 gather_fusion
  98.7 0.1 compare_and_fusion
  98.8 0.1 broadcast_select_fusion
  98.8 16.1 %all-to-all-done.1 = bf16[16,2,16,512]{3,2,1,0:T(8,128)(2,1)S(1)} async-done(((bf16[16,2,16,512]{3,2,1,0:T(8,128)(2,1)}), bf16[16,2,16,512]{3,2,1,0:T(8,128)(2,1)S(1)}, u32[]{:S(2)}, u32[]{:S(2)}) %all-to-all-start.1) | async-done | bytes 524320 | tf_op jit(solution)/shard_map/all_to_all | solution.py:18
  114.9 0.1 convert_reduce_fusion
  115.0 0.9 broadcast_in_dim.11
  115.9 19.8 %all-to-all-start.2 = ((bf16[16,2,16,512]{3,2,1,0:T(8,128)(2,1)}), bf16[16,2,16,512]{3,2,1,0:T(8,128)(2,1)S(1)}, u32[]{:S(2)}, u32[]{:S(2)}) async-start(bf16[16,2,16,512]{3,2,1,0:T(8,128)(2,1)} %broadcast_in_dim.11), calls=%async_computation.2 | async-start | bytes 1048576 | tf_op jit(solution)/shard_map/all_to_all | solution.py:30
  135.7 0.0 all-gather.2.cloned.1.call-start
  135.8 4.6 %fusion.45 = (bf16[256,1024]{1,0:T(8,128)(2,1)S(1)}, bf16[256,1024]{1,0:T(8,128)(2,1)S(1)}, bf16[256,1024]{1,0:T(8,128)(2,1)S(1)}) fusion(s32[1024]{0:T(1024)S(1)} %iota_add_fusion, s32[256]{0:T(256)S(1)} %iota_multiply_fusion), kind=kLoop, calls=%fused_computation.84 | loop fusion | flops 5242880 | bytes 1577984 | tf_op jit(solution)/shard_map/convert.9
  140.4 24.2 %all-to-all-done.2 = bf16[16,2,16,512]{3,2,1,0:T(8,128)(2,1)S(1)} async-done(((bf16[16,2,16,512]{3,2,1,0:T(8,128)(2,1)}), bf16[16,2,16,512]{3,2,1,0:T(8,128)(2,1)S(1)}, u32[]{:S(2)}, u32[]{:S(2)}) %all-to-all-start.2) | async-done | bytes 524320 | tf_op jit(solution)/shard_map/all_to_all | solution.py:30
  164.6 1.3 fusion.11
  165.8 0.7 subtract_reduce_fusion
  166.5 0.6 pad_maximum_fusion.1
  167.1 0.0 all-gather.2.cloned.1.call-update
  167.2 0.0 copy-start.1
  167.2 0.0 copy-start.2
  167.2 60.1 %all-gather.2.cloned.1.call-done = bf16[512,2048]{1,0:T(8,128)(2,1)} async-done(((bf16[16,2048]{1,0:T(8,128)(2,1)}), bf16[512,2048]{1,0:T(8,128)(2,1)}) %all-gather.2.cloned.1.call-update) | async-done | bytes 2097168 | tf_op jit(solution)/shard_map/all_gather | solution.py:143
  227.2 1.7 fusion.56
  228.9 0.0 copy-done.1
  229.0 0.0 copy-done.2
  229.0 2.6 %fusion.18 = f32[512,1024]{1,0:T(8,128)} fusion(bf16[512,1024]{1,0:T(8,128)(2,1)S(1)} %get-tuple-element.8, bf16[512,1024]{1,0:T(8,128)(2,1)S(1)} %get-tuple-element.7, bf16[512,512]{1,0:T(8,128)(2,1)S(1)} %copy-done.2, bf16[512,512]{1,0:T(8,128)(2,1)S(1)} %copy-done.1), kind=kOutput, calls=%fused_computation.24 | convolution fusion | flops 1080033280 | bytes 5242880 | tf_op jit(solution)/shard_map/dot_general | solution.py:148
  (8 shorter events, 0.1 us)
Async XLA Ops:
  6.5 10.7 %copy-start = (bf16[512,1024]{1,0:T(8,128)(2,1)S(1)}, bf16[512,1024]{1,0:T(8,128)(2,1)}, u32[]{:S(2)}) copy-start(bf16[512,1024]{1,0:T(8,128)(2,1)} %param.5) | copy-start | bytes 3145732
  20.4 10.7 %copy-start.7 = (s32[2,32]{1,0:T(2,128)S(1)}, s32[2,32]{1,0:T(2,128)}, u32[]{:S(2)}) copy-start(s32[2,32]{1,0:T(2,128)} %param.8) | copy-start | bytes 772
  20.4 58.7 %all-to-all-start = ((bf16[32,16,2048]{2,1,0:T(8,128)(2,1)}), bf16[32,16,2048]{2,1,0:T(8,128)(2,1)S(1)}, u32[]{:S(2)}, u32[]{:S(2)}) async-start(bf16[32,16,2048]{2,1,0:T(8,128)(2,1)} %pad_maximum_fusion), calls=%async_computation | async-start | bytes 4194304 | tf_op jit(solution)/shard_map/all_to_all | solution.py:18
  79.5 1.0 copy-start.3
  79.5 1.2 copy-start.4
  79.5 1.3 copy-start.5
  80.8 16.3 %copy-start.6 = (s32[2,32]{1,0:T(2,128)S(1)}, s32[2,32]{1,0:T(2,128)}, u32[]{:S(2)}) copy-start(s32[2,32]{1,0:T(2,128)} %param.9) | copy-start | bytes 772
  82.9 32.1 %all-to-all-start.1 = ((bf16[16,2,16,512]{3,2,1,0:T(8,128)(2,1)}), bf16[16,2,16,512]{3,2,1,0:T(8,128)(2,1)S(1)}, u32[]{:S(2)}, u32[]{:S(2)}) async-start(bf16[16,2,16,512]{3,2,1,0:T(8,128)(2,1)} %bitcast.4), calls=%async_computation.1 | async-start | bytes 1048576 | tf_op jit(solution)/shard_map/all_to_all | solution.py:18
  115.9 48.7 %all-to-all-start.2 = ((bf16[16,2,16,512]{3,2,1,0:T(8,128)(2,1)}), bf16[16,2,16,512]{3,2,1,0:T(8,128)(2,1)S(1)}, u32[]{:S(2)}, u32[]{:S(2)}) async-start(bf16[16,2,16,512]{3,2,1,0:T(8,128)(2,1)} %broadcast_in_dim.11), calls=%async_computation.2 | async-start | bytes 1048576 | tf_op jit(solution)/shard_map/all_to_all | solution.py:30
  135.7 91.5 %all-gather.2.cloned.1.call-start = ((), (), s32[]{:S(2)}) async-start(), calls=%async_computation.3 | async-start | bytes 2162688 | tf_op jit(solution)/shard_map/all_gather | solution.py:143
  167.2 61.8 %copy-start.1 = (bf16[512,512]{1,0:T(8,128)(2,1)S(1)}, bf16[512,512]{1,0:T(8,128)(2,1)}, u32[]{:S(2)}) copy-start(bf16[512,512]{1,0:T(8,128)(2,1)} %get-tuple-element.21) | copy-start | bytes 1572868
  167.2 61.8 %copy-start.2 = (bf16[512,512]{1,0:T(8,128)(2,1)S(1)}, bf16[512,512]{1,0:T(8,128)(2,1)}, u32[]{:S(2)}) copy-start(bf16[512,512]{1,0:T(8,128)(2,1)} %get-tuple-element.22) | copy-start | bytes 1572868
Sparse Core Ops, SparseCore 0:
  167.3 59.9 all-gather.1
where the time goes:
time: 239 us; the launch traced here: 238 us
  waiting for transfers between devices  142 us (59%)
  starting transfers between devices  44.7 us (19%)
  other arithmetic  26.2 us (11%)
  between operations  13.6 us (6%)
  matrix products  7.13 us (3%)
  local copies, waits for them, and re-layouts  4.74 us (2%)
    all_gather x1, waiting for transfers between devices, body(): shards = lax.all_gather(strip_image, 'frow', axis=0, tiled=True)  60.1 us
    all_to_all x2, waiting for transfers between devices, sent_and_summed(): parts = lax.all_to_all(split_up(value, dim, length), axis, 0, 0, tiled=True)  57.7 us
    all_to_all x2, starting transfers between devices, sent_and_summed(): parts = lax.all_to_all(split_up(value, dim, length), axis, 0, 0, tiled=True)  24.9 us
    all_to_all x1, waiting for transfers between devices, copy_for_each(): return lax.all_to_all(copies, axis, split_axis=0, concat_axis=0, tiled=True)  24.2 us
    another operation x5, other arithmetic  21.3 us
    all_to_all x1, starting transfers between devices, copy_for_each(): return lax.all_to_all(copies, axis, split_axis=0, concat_axis=0, tiled=True)  19.8 us
  transfers between devices with their start and end apart: 4, of which 4 were waited for; matrix products, arithmetic and copies ran while one was open for 5% of the time, Pallas kernels for 0%

commit v1 on v0

--- a/solution.py
+++ b/solution.py
@@ -140,7 +140,9 @@
     spectra = spectra.reshape(shards.shape[0], share_rows, 2 * facet_width)
     merged = demodulate(spectra, cos_shift, sin_shift, facet_width)
     strip_image = merged.astype(jnp.bfloat16)
-    shards = lax.all_gather(strip_image, "frow", axis=0, tiled=True)
+    shards = jnp.concatenate(
+        lax.all_to_all(jnp.stack([strip_image] * lax.axis_size("frow")), "frow", 0, 0), axis=0
+    )
     wanted = frequencies
     cosine, sine = phase_pair(pixel_rows, wanted, modulus, row_scale)
     phases = jnp.concatenate([cosine, -sine], axis=1).astype(jnp.bfloat16)

time: 239 us -> 222 us (0.929)
  waiting for transfers between devices: 142 us -> 81.9 us
  blocking collectives: 0 us -> 57.2 us
  between operations: 13.6 us -> 0.24 us
    all_gather x1 -> x0, waiting for transfers between devices: 60.1 us -> none  [body(): shards = lax.all_gather(strip_image, 'frow', axis=0, tiled=True)]
    all_to_all x0 -> x1, blocking collectives: none -> 57.2 us  [body(): lax.all_to_all(jnp.stack([strip_image] * lax.axis_size('frow')), 'frow',...]
  transfers between devices with their start and end apart: 4 -> 3, of which waited for: 4 -> 3; matrix products, arithmetic and copies ran while one was open for 5% -> 6% of each run, Pallas kernels for 0% -> 0%
where the time goes in v1:
time: 222 us; the launch traced here: 221 us
  waiting for transfers between devices  81.9 us (37%)
  blocking collectives  57.2 us (26%)
  starting transfers between devices  44.7 us (20%)
  other arithmetic  25.6 us (12%)
  matrix products  7.12 us (3%)
  local copies, waits for them, and re-layouts  4.45 us (2%)
    all_to_all x2, waiting for transfers between devices, sent_and_summed(): parts = lax.all_to_all(split_up(value, dim, length), axis, 0, 0, tiled=True)  57.6 us
    all_to_all x1, blocking collectives, body(): lax.all_to_all(jnp.stack([strip_image] * lax.axis_size('frow')), 'frow',...  57.2 us
    all_to_all x2, starting transfers between devices, sent_and_summed(): parts = lax.all_to_all(split_up(value, dim, length), axis, 0, 0, tiled=True)  24.9 us
    all_to_all x1, waiting for transfers between devices, copy_for_each(): return lax.all_to_all(copies, axis, split_axis=0, concat_axis=0, tiled=True)  24.3 us
    another operation x5, other arithmetic  21.3 us
    all_to_all x1, starting transfers between devices, copy_for_each(): return lax.all_to_all(copies, axis, split_axis=0, concat_axis=0, tiled=True)  19.8 us
  transfers between devices with their start and end apart: 3, of which 3 were waited for; matrix products, arithmetic and copies ran while one was open for 6% of the time, Pallas kernels for 0%

profile of v1, /device:TPU:1, one launch (start us, length us, event | category | flops | bytes accessed | tf_op | source)
XLA Modules:
  0.0 221.2 jit_solution(4029756052198464532)
XLA Ops:
  0.0 0.0 copy-start
  0.0 0.8 add_bitcast_fusion
  0.8 9.9 %multiply_convert_fusion.4 = (bf16[512,512]{1,0:T(8,128)(2,1)}, bf16[512,512]{1,0:T(8,128)(2,1)}, bf16[512,512]{1,0:T(8,128)(2,1)S(1)}, bf16[512,512]{1,0:T(8,128)(2,1)S(1)}) fusion(s32[512]{0:T(512)S(1)} %bitcast.30, s32[512]{0:T(512)S(1)} %iota_add_fusion.1), kind=kLoop, calls=%fused_computation.82 | loop fusion | flops 9699328 | bytes 2101248 | tf_op jit(solution)/shard_map/convert.25
  10.7 0.0 copy-done
  10.7 1.3 fusion.40
  12.0 0.2 slice.53
  12.1 0.3 fusion
  12.4 1.5 pad_maximum_fusion
  13.9 0.0 copy-start.7
  13.9 10.6 %all-to-all-start = ((bf16[32,16,2048]{2,1,0:T(8,128)(2,1)}), bf16[32,16,2048]{2,1,0:T(8,128)(2,1)S(1)}, u32[]{:S(2)}, u32[]{:S(2)}) async-start(bf16[32,16,2048]{2,1,0:T(8,128)(2,1)} %pad_maximum_fusion), calls=%async_computation | async-start | bytes 4194304 | tf_op jit(solution)/shard_map/all_to_all | solution.py:18
  24.6 0.0 copy-done.7
  24.6 0.6 fusion.50
  25.2 5.9 %negate_convert_fusion.1 = (bf16[1024,256]{1,0:T(8,128)(2,1)}, bf16[1024,256]{1,0:T(8,128)(2,1)}, bf16[1024,256]{1,0:T(8,128)(2,1)}) fusion(s32[256]{0:T(256)S(1)} %iota_multiply_fusion, s32[1024]{0:T(1024)S(1)} %iota_add_fusion), kind=kLoop, calls=%fused_computation.76 | loop fusion | flops 5242880 | bytes 1577984 | tf_op jit(solution)/shard_map/convert.15
  31.1 41.5 %all-to-all-done = bf16[32,16,2048]{2,1,0:T(8,128)(2,1)S(1)} async-done(((bf16[32,16,2048]{2,1,0:T(8,128)(2,1)}), bf16[32,16,2048]{2,1,0:T(8,128)(2,1)S(1)}, u32[]{:S(2)}, u32[]{:S(2)}) %all-to-all-start) | async-done | bytes 2097184 | tf_op jit(solution)/shard_map/all_to_all | solution.py:18
  72.6 0.3 reduce_sum.39
  72.9 0.0 copy-start.3
  73.0 0.0 copy-start.4
  73.0 0.0 copy-start.5
  73.0 0.7 add_convert_fusion
  73.7 0.3 copy-done.3
  74.0 0.2 copy-done.4
  74.1 0.2 copy-done.5
  74.3 0.0 copy-start.6
  74.3 2.0 fusion.22
  76.4 14.2 %all-to-all-start.1 = ((bf16[16,2,16,512]{3,2,1,0:T(8,128)(2,1)}), bf16[16,2,16,512]{3,2,1,0:T(8,128)(2,1)S(1)}, u32[]{:S(2)}, u32[]{:S(2)}) async-start(bf16[16,2,16,512]{3,2,1,0:T(8,128)(2,1)} %bitcast.4), calls=%async_computation.1 | async-start | bytes 1048576 | tf_op jit(solution)/shard_map/all_to_all | solution.py:18
  90.6 0.0 copy-done.6
  90.6 0.1 fusion.51
  90.7 0.8 constant_dynamic-slice_fusion
  91.6 0.5 gather_fusion
  92.1 0.1 compare_and_fusion
  92.2 0.1 broadcast_select_fusion
  92.3 16.1 %all-to-all-done.1 = bf16[16,2,16,512]{3,2,1,0:T(8,128)(2,1)S(1)} async-done(((bf16[16,2,16,512]{3,2,1,0:T(8,128)(2,1)}), bf16[16,2,16,512]{3,2,1,0:T(8,128)(2,1)S(1)}, u32[]{:S(2)}, u32[]{:S(2)}) %all-to-all-start.1) | async-done | bytes 524320 | tf_op jit(solution)/shard_map/all_to_all | solution.py:18
  108.4 0.1 convert_reduce_fusion
  108.5 0.9 broadcast_in_dim.11
  109.4 19.8 %all-to-all-start.2 = ((bf16[16,2,16,512]{3,2,1,0:T(8,128)(2,1)}), bf16[16,2,16,512]{3,2,1,0:T(8,128)(2,1)S(1)}, u32[]{:S(2)}, u32[]{:S(2)}) async-start(bf16[16,2,16,512]{3,2,1,0:T(8,128)(2,1)} %broadcast_in_dim.11), calls=%async_computation.2 | async-start | bytes 1048576 | tf_op jit(solution)/shard_map/all_to_all | solution.py:30
  129.2 4.6 %fusion.45 = (bf16[256,1024]{1,0:T(8,128)(2,1)S(1)}, bf16[256,1024]{1,0:T(8,128)(2,1)S(1)}, bf16[256,1024]{1,0:T(8,128)(2,1)S(1)}) fusion(s32[1024]{0:T(1024)S(1)} %iota_add_fusion, s32[256]{0:T(256)S(1)} %iota_multiply_fusion), kind=kLoop, calls=%fused_computation.84 | loop fusion | flops 5242880 | bytes 1577984 | tf_op jit(solution)/shard_map/convert.9
  133.8 24.3 %all-to-all-done.2 = bf16[16,2,16,512]{3,2,1,0:T(8,128)(2,1)S(1)} async-done(((bf16[16,2,16,512]{3,2,1,0:T(8,128)(2,1)}), bf16[16,2,16,512]{3,2,1,0:T(8,128)(2,1)S(1)}, u32[]{:S(2)}, u32[]{:S(2)}) %all-to-all-start.2) | async-done | bytes 524320 | tf_op jit(solution)/shard_map/all_to_all | solution.py:30
  158.0 1.3 fusion.11
  159.3 0.7 subtract_reduce_fusion
  160.0 0.2 stack.2
  160.2 57.2 %all_to_all.20 = bf16[32,16,2048]{2,1,0:T(8,128)(2,1)S(1)} all-to-all(bf16[32,16,2048]{2,1,0:T(8,128)(2,1)S(1)} %stack.2), channel_id=1, replica_groups=mesh['frow'=32,'fcol'=16] {'frow'}, dimensions={0} | all-to-all | bytes 4194304 | tf_op jit(solution)/shard_map/all_to_all | solution.py:144
  217.4 0.0 copy-start.1
  217.4 0.0 copy-start.2
  217.4 0.2 fusion.56
  217.6 0.8 copy-done.1
  218.5 0.2 copy-done.2
  218.6 2.6 %fusion.18 = f32[512,1024]{1,0:T(8,128)} fusion(bf16[512,1024]{1,0:T(8,128)(2,1)S(1)} %get-tuple-element.8, bf16[512,1024]{1,0:T(8,128)(2,1)S(1)} %get-tuple-element.7, bf16[512,512]{1,0:T(8,128)(2,1)S(1)} %copy-done.2, bf16[512,512]{1,0:T(8,128)(2,1)S(1)} %copy-done.1), kind=kOutput, calls=%fused_computation.24 | convolution fusion | flops 1080033280 | bytes 5242880 | tf_op jit(solution)/shard_map/dot_general | solution.py:150
  (9 shorter events, 0.1 us)
Async XLA Ops:
  0.0 10.7 %copy-start = (bf16[512,1024]{1,0:T(8,128)(2,1)S(1)}, bf16[512,1024]{1,0:T(8,128)(2,1)}, u32[]{:S(2)}) copy-start(bf16[512,1024]{1,0:T(8,128)(2,1)} %param.5) | copy-start | bytes 3145732
  13.9 10.7 %copy-start.7 = (s32[2,32]{1,0:T(2,128)S(1)}, s32[2,32]{1,0:T(2,128)}, u32[]{:S(2)}) copy-start(s32[2,32]{1,0:T(2,128)} %param.8) | copy-start | bytes 772
  13.9 58.7 %all-to-all-start = ((bf16[32,16,2048]{2,1,0:T(8,128)(2,1)}), bf16[32,16,2048]{2,1,0:T(8,128)(2,1)S(1)}, u32[]{:S(2)}, u32[]{:S(2)}) async-start(bf16[32,16,2048]{2,1,0:T(8,128)(2,1)} %pad_maximum_fusion), calls=%async_computation | async-start | bytes 4194304 | tf_op jit(solution)/shard_map/all_to_all | solution.py:18
  72.9 1.0 copy-start.3
  73.0 1.2 copy-start.4
  73.0 1.3 copy-start.5
  74.3 16.3 %copy-start.6 = (s32[2,32]{1,0:T(2,128)S(1)}, s32[2,32]{1,0:T(2,128)}, u32[]{:S(2)}) copy-start(s32[2,32]{1,0:T(2,128)} %param.9) | copy-start | bytes 772
  76.4 32.1 %all-to-all-start.1 = ((bf16[16,2,16,512]{3,2,1,0:T(8,128)(2,1)}), bf16[16,2,16,512]{3,2,1,0:T(8,128)(2,1)S(1)}, u32[]{:S(2)}, u32[]{:S(2)}) async-start(bf16[16,2,16,512]{3,2,1,0:T(8,128)(2,1)} %bitcast.4), calls=%async_computation.1 | async-start | bytes 1048576 | tf_op jit(solution)/shard_map/all_to_all | solution.py:18
  109.4 48.7 %all-to-all-start.2 = ((bf16[16,2,16,512]{3,2,1,0:T(8,128)(2,1)}), bf16[16,2,16,512]{3,2,1,0:T(8,128)(2,1)S(1)}, u32[]{:S(2)}, u32[]{:S(2)}) async-start(bf16[16,2,16,512]{3,2,1,0:T(8,128)(2,1)} %broadcast_in_dim.11), calls=%async_computation.2 | async-start | bytes 1048576 | tf_op jit(solution)/shard_map/all_to_all | solution.py:30
  217.4 1.0 copy-start.1
  217.4 1.2 copy-start.2
